TPU v7x, 128 devices: a whole 4x4x4 slice. The times are simulated.
128 devices in a mesh: ctx: 16 (over y, z), wt: 8 (over x, core).
Axes of the slice: x: 4, y: 4, z: 4, core: 2. Of those that a mesh axis runs over, the one named last changes fastest.
Arguments:
- frames: bfloat16 [1024, 1280], P('wt'), may hold values from -6 to 6
- span_source: int32 [64], P('wt'), may hold values from 0 to 7, as said below
- adapter_weight: bfloat16 [1280, 4096], P(None, 'ctx'), may hold values from -0.15625 to 0.15625
- adapter_bias: float32 [4096], P('ctx'), may hold values from -3 to 3
- norm_gain: float32 [4096], replicated, may hold values from 0.25 to 1.75
- qkv_weight: bfloat16 [4096, 3, 4096], P('wt', None, 'ctx'), may hold values from -0.09375 to 0.09375
- out_weight: bfloat16 [4096, 4096], P('ctx', 'wt'), may hold values from -0.125 to 0.125
- k_cache: bfloat16 [16, 2048, 4096], P('wt', 'ctx'), may hold values from -600 to 600
- v_cache: bfloat16 [16, 2048, 4096], P('wt', 'ctx'), may hold values from -12 to 12
- lengths: int32 [16], P('wt'), may hold values from 1 to 2048
Outputs:
- attn_out: bfloat16 [1024, 4096], P('wt', 'ctx')
- new_keys: bfloat16 [1024, 4096], P('wt', 'ctx')
- new_values: bfloat16 [1024, 4096], P('wt', 'ctx')
Inputs may be any that keep to these rules, and one draw needn't show every extreme that they name: `span_source`: each aligned block of 8 entries is a permutation of 0 to 7.
All inputs are finite; a program needn't handle non-finite values.
Results may differ from a plain program's by a relative error of at most 0.02.
Values may be sent and summed in bfloat16 or wider, within the bound.
No kernel may reach another device: no remote copies, remote signals or barrier semaphores. Data moves between devices by JAX's collectives and lax.ppermute only.
A program may use at most 64 MiB of HBM per device.

v0:
```python
import jax
import jax.numpy as jnp
from jax import lax
from jax.sharding import PartitionSpec as P

HEADS = 32
HEAD = 128
FLOOR_SCORE = -1e30


def in_order(blocks, dim):
    lengths = list(blocks.shape[1:])
    lengths[dim] *= blocks.shape[0]
    return jnp.moveaxis(blocks, 0, dim).reshape(lengths)


def from_everyone(x, axis):
    count = lax.axis_size(axis)
    return lax.all_to_all(jnp.broadcast_to(x[None], (count, *x.shape)), axis, 0, 0, tiled=True)


def gather_directly(x, axis, dim):
    return in_order(from_everyone(x, axis), dim)


def cut_along(x, dim, count):
    before, after = (x.shape[:dim], x.shape[dim + 1 :])
    return jnp.moveaxis(x.reshape(*before, count, -1, *after), dim, 0)


def summed_on_arrival(x, axis, dim):
    count = lax.axis_size(axis)
    blocks = lax.all_to_all(cut_along(x, dim, count), axis, 0, 0, tiled=True)
    return jnp.sum(blocks.astype(jnp.float32), axis=0)


def rotate(values, positions):
    half = values.shape[-1] // 2
    freq = 10000.0 ** (-2.0 * jnp.arange(half, dtype=jnp.float32) / values.shape[-1])
    angle = positions.astype(jnp.float32)[:, None] * freq[None, :]
    cosine = jnp.cos(angle)[:, None, :]
    sine = jnp.sin(angle)[:, None, :]
    first = values[..., :half]
    second = values[..., half:]
    return jnp.concatenate(
        [first * cosine - second * sine, second * cosine + first * sine], axis=-1
    )


def combine_parts(left, right):
    left_max, left_total, left_numer = left
    right_max, right_total, right_numer = right
    joint = jnp.maximum(left_max, right_max)
    left_scale = jnp.exp(left_max - joint)
    right_scale = jnp.exp(right_max - joint)
    return (
        joint,
        left_total * left_scale + right_total * right_scale,
        left_numer * left_scale[..., None] + right_numer * right_scale[..., None],
    )


def finish_heads(parts):
    shard_max, shard_total, shard_numer = parts
    joint = jnp.max(shard_max, axis=0)
    factor = jnp.exp(shard_max - joint[None])
    total = jnp.sum(shard_total * factor, axis=0)
    numer = jnp.sum(shard_numer * factor[..., None], axis=0)
    return (numer / total[..., None]).astype(jnp.bfloat16)


def shards(
    frames,
    span_source,
    adapter_weight,
    adapter_bias,
    norm_gain,
    qkv_weight,
    out_weight,
    k_cache,
    v_cache,
    lengths,
):
    tok_rows, audio_width = frames.shape
    group_spans = span_source.shape[0]
    span_len = tok_rows // group_spans
    meet_count = lengths.shape[0]
    new_count = tok_rows // meet_count
    hist_local = k_cache.shape[1]
    cols_local = qkv_weight.shape[2]
    heads_here = cols_local // HEAD
    scale = HEAD ** (-0.5)
    ctx_rank = lax.axis_index("ctx")
    head_start = ctx_rank * heads_here
    ordered = frames.reshape(group_spans, span_len, audio_width)[span_source].reshape(
        tok_rows, audio_width
    )
    adapted = (
        jnp.dot(ordered, adapter_weight, preferred_element_type=jnp.float32) + adapter_bias
    ).astype(jnp.bfloat16)
    features = gather_directly(adapted, "ctx", 1)
    wide = features.astype(jnp.float32)
    normed = (
        wide * lax.rsqrt(jnp.mean(wide * wide, axis=-1, keepdims=True) + 1e-06) * norm_gain
    ).astype(jnp.bfloat16)
    qkv_full, out_rows = (
        lax.all_gather(qkv_weight, "wt", axis=0, tiled=True),
        lax.all_gather(out_weight, "wt", axis=1, tiled=True),
    )
    projected = jnp.einsum("rd,dke->rke", normed, qkv_full, preferred_element_type=jnp.float32)
    positions = (lengths[:, None] + jnp.arange(new_count, dtype=jnp.int32)[None, :]).reshape(
        tok_rows
    )
    query_local = rotate(projected[:, 0].reshape(tok_rows, heads_here, HEAD), positions).astype(
        jnp.bfloat16
    )
    key_local = rotate(projected[:, 1].reshape(tok_rows, heads_here, HEAD), positions).astype(
        jnp.bfloat16
    )
    value_local = projected[:, 2].reshape(tok_rows, heads_here, HEAD).astype(jnp.bfloat16)
    query_every = gather_directly(query_local.reshape(tok_rows, cols_local), "ctx", 1)
    query_heads = query_every.reshape(meet_count, new_count, HEADS, HEAD)
    keys_hist = k_cache.reshape(meet_count, hist_local, HEADS, HEAD)
    vals_hist = v_cache.reshape(meet_count, hist_local, HEADS, HEAD)
    scores = (
        jnp.einsum("mthd,mphd->mhtp", query_heads, keys_hist, preferred_element_type=jnp.float32)
        * scale
    )
    key_place = ctx_rank * hist_local + jnp.arange(hist_local, dtype=jnp.int32)
    live = (key_place[None, :] < lengths[:, None])[:, None, None, :]
    hist_max = jnp.maximum(jnp.max(jnp.where(live, scores, -jnp.inf), axis=-1), FLOOR_SCORE)
    hist_weights = jnp.where(live, jnp.exp(scores - hist_max[..., None]), 0.0)
    hist_total = jnp.sum(hist_weights, axis=-1)
    hist_numer = jnp.einsum(
        "mhtp,mphd->mthd",
        hist_weights.astype(jnp.bfloat16),
        vals_hist,
        preferred_element_type=jnp.float32,
    ).reshape(tok_rows, HEADS, HEAD)
    hist_max = jnp.transpose(hist_max, (0, 2, 1)).reshape(tok_rows, HEADS)
    hist_total = jnp.transpose(hist_total, (0, 2, 1)).reshape(tok_rows, HEADS)
    query_new = query_local.reshape(meet_count, new_count, heads_here, HEAD)
    key_new = key_local.reshape(meet_count, new_count, heads_here, HEAD)
    value_new = value_local.reshape(meet_count, new_count, heads_here, HEAD)
    new_scores = (
        jnp.einsum("mthd,mshd->mhts", query_new, key_new, preferred_element_type=jnp.float32)
        * scale
    )
    causal = (
        jnp.arange(new_count, dtype=jnp.int32)[:, None]
        >= jnp.arange(new_count, dtype=jnp.int32)[None, :]
    )[None, None]
    new_max = jnp.max(jnp.where(causal, new_scores, -jnp.inf), axis=-1)
    new_weights = jnp.where(causal, jnp.exp(new_scores - new_max[..., None]), 0.0)
    new_total = jnp.sum(new_weights, axis=-1)
    new_numer = jnp.einsum(
        "mhts,mshd->mthd",
        new_weights.astype(jnp.bfloat16),
        value_new,
        preferred_element_type=jnp.float32,
    ).reshape(tok_rows, heads_here, HEAD)
    new_max = jnp.transpose(new_max, (0, 2, 1)).reshape(tok_rows, heads_here)
    new_total = jnp.transpose(new_total, (0, 2, 1)).reshape(tok_rows, heads_here)
    own_part = (
        lax.dynamic_slice_in_dim(hist_max, head_start, heads_here, 1),
        lax.dynamic_slice_in_dim(hist_total, head_start, heads_here, 1),
        lax.dynamic_slice_in_dim(hist_numer, head_start, heads_here, 1),
    )
    joined_max, joined_total, joined_numer = combine_parts(
        own_part, (new_max, new_total, new_numer)
    )
    part_max = lax.dynamic_update_slice_in_dim(hist_max, joined_max, head_start, 1)
    part_total = lax.dynamic_update_slice_in_dim(hist_total, joined_total, head_start, 1)
    part_numer = lax.dynamic_update_slice_in_dim(hist_numer, joined_numer, head_start, 1)
    attended = finish_heads(
        (
            lax.all_to_all(
                part_max[None].astype(jnp.bfloat16), "ctx", split_axis=2, concat_axis=0, tiled=True
            ).astype(jnp.float32),
            lax.all_to_all(
                part_total[None].astype(jnp.bfloat16),
                "ctx",
                split_axis=2,
                concat_axis=0,
                tiled=True,
            ).astype(jnp.float32),
            lax.all_to_all(
                part_numer[None].astype(jnp.bfloat16),
                "ctx",
                split_axis=2,
                concat_axis=0,
                tiled=True,
            ).astype(jnp.float32),
        )
    )
    attended_flat = attended.reshape(tok_rows, cols_local)
    out_terms = jnp.dot(attended_flat, out_rows, preferred_element_type=jnp.float32)
    attn_out = summed_on_arrival(out_terms.astype(jnp.bfloat16), "ctx", 1).astype(jnp.bfloat16)
    return (
        attn_out,
        key_local.reshape(tok_rows, cols_local),
        value_local.reshape(tok_rows, cols_local),
    )


def solution(mesh):
    return jax.shard_map(
        shards,
        mesh=mesh,
        in_specs=(
            P("wt", None),
            P("wt"),
            P(None, "ctx"),
            P("ctx"),
            P(),
            P("wt", None, "ctx"),
            P("ctx", "wt"),
            P("wt", "ctx", None),
            P("wt", "ctx", None),
            P("wt"),
        ),
        out_specs=(P("wt", "ctx"), P("wt", "ctx"), P("wt", "ctx")),
        check_vma=False,
    )
```

profile of v0, /device:TPU:0, one launch (start us, length us, event | category | flops | bytes accessed | tf_op | source)
XLA Modules:
  0.0 184.5 jit_solution(12653421119872062903)
XLA Ops:
  12.6 8.2 %all-to-all-start = ((bf16[16,128,256]{2,1,0:T(8,128)(2,1)}), bf16[16,128,256]{2,1,0:T(8,128)(2,1)}, u32[]{:S(2)}, u32[]{:S(2)}) async-start(bf16[16,128,256]{2,1,0:T(8,128)(2,1)} %broadcast_in_dim.95), calls=%async_computation | async-start | bytes 2097152 | tf_op jit(solution)/shard_map/all_to_all | solution.py:19
  21.9 16.7 %all-to-all-done = bf16[16,128,256]{2,1,0:T(8,128)(2,1)} async-done(((bf16[16,128,256]{2,1,0:T(8,128)(2,1)}), bf16[16,128,256]{2,1,0:T(8,128)(2,1)}, u32[]{:S(2)}, u32[]{:S(2)}) %all-to-all-start) | async-done | bytes 1048608 | tf_op jit(solution)/shard_map/all_to_all | solution.py:19
  38.6 1.6 copy.143
  42.3 10.7 %all-gather.3.cloned.1.call-done = bf16[4096,3,256]{2,0,1:T(8,128)(2,1)} async-done(((bf16[512,3,256]{2,0,1:T(8,128)(2,1)}), bf16[4096,3,256]{2,0,1:T(8,128)(2,1)}) %all-gather.3.cloned.1.call-update) | async-done | bytes 6291472 | tf_op jit(solution)/shard_map/all_gather | solution.py:107
  53.0 4.2 %fusion.16 = f32[128,3,256]{2,0,1:T(8,128)S(1)} fusion(bf16[4096,3,256]{2,0,1:T(8,128)(2,1)} %all-gather.3.cloned.1.call-done, bf16[128,4096]{0,1:T(8,128)(2,1)} %fusion.8), kind=kOutput, calls=%fused_computation.24 | convolution fusion | flops 805306368 | bytes 7733248 | tf_op jit(solution)/shard_map/rd,dke->rke/dot_general | solution.py:110
  59.9 7.0 %all-to-all-start.1 = ((bf16[16,128,256]{2,1,0:T(8,128)(2,1)}), bf16[16,128,256]{2,1,0:T(8,128)(2,1)S(1)}, u32[]{:S(2)}, u32[]{:S(2)}) async-start(bf16[16,128,256]{2,1,0:T(8,128)(2,1)} %broadcast_in_dim.96), calls=%async_computation.1 | async-start | bytes 2097152 | tf_op jit(solution)/shard_map/all_to_all | solution.py:19
  76.5 1.6 copy.159
  78.1 1.6 copy.160
  79.7 1.8 select_reduce_fusion.1
  92.7 2.9 %select_reduce_fusion = (f32[2,32,64]{2,1,0:T(8,128)S(1)}, f32[2,32,64,128]{3,2,1,0:T(8,128)}) fusion(pred[2,128]{1,0:T(4,128)(4,1)S(1)} %copy-done.9, bf16[2,64,32,128]{3,2,1,0:T(8,128)(2,1)S(1)} %reshape_reshape.3, bf16[2,128,4096]{2,1,0:T(8,128)(2,1)S(1)} %copy-done), kind=kOutput, calls=%fused_computation.14 | convolution fusion | flops 135786496 | bytes 5259520 | tf_op jit(solution)/shard_map/mthd,mphd->mhtp/dot_general | solution.py:126
  95.8 2.5 %fusion.12 = f32[2,32,64]{2,1,0:T(8,128)S(1)} fusion(f32[2,32,64,128]{3,2,1,0:T(8,128)} %get-tuple-element.21, f32[2,32,64]{2,1,0:T(8,128)S(1)} %get-tuple-element.15, pred[2,128]{1,0:T(4,128)(4,1)S(1)} %copy-done.9), kind=kLoop, calls=%fused_computation.17 | loop fusion | flops 2093056 | bytes 2130176 | tf_op jit(solution)/shard_map/reduce_sum | solution.py:133
  99.2 7.2 %all-to-all-start.3 = ((bf16[16,2,128]{2,1,0:T(2,128)(2,1)}), bf16[16,2,128]{2,1,0:T(2,128)(2,1)S(1)}, u32[]{:S(2)}, u32[]{:S(2)}) async-start(bf16[16,2,128]{2,1,0:T(2,128)(2,1)} %bitcast.125), calls=%async_computation.3 | async-start | bytes 16384 | tf_op jit(solution)/shard_map/all_to_all | solution.py:177
  106.4 4.3 %fusion.9 = f32[2,64,32,128]{3,1,2,0:T(8,128)} fusion(f32[2,32,64,128]{3,2,1,0:T(8,128)} %get-tuple-element.21, f32[2,32,64]{2,1,0:T(8,128)S(1)} %get-tuple-element.15, pred[2,128]{1,0:T(4,128)(4,1)S(1)} %copy-done.9, bf16[2,128,4096]{2,1,0:T(8,128)(2,1)} %param.18), kind=kOutput, calls=%fused_computation.16 | convolution fusion | flops 136314880 | bytes 6308096 | tf_op jit(solution)/shard_map/mhtp,mphd->mthd/dot_general | solution.py:134
  111.5 2.8 %copy.152 = f32[2,64,32,128]{3,2,1,0:T(8,128)S(1)} copy(f32[2,64,32,128]{3,1,2,0:T(8,128)} %fusion.9) | data formatting | bytes 4194304 | tf_op jit(solution)/shard_map/mhtp,mphd->mthd/transpose | solution.py:134
  117.0 7.2 %all-to-all-start.4 = ((bf16[16,2,128]{2,1,0:T(2,128)(2,1)}), bf16[16,2,128]{2,1,0:T(2,128)(2,1)S(1)}, u32[]{:S(2)}, u32[]{:S(2)}) async-start(bf16[16,2,128]{2,1,0:T(2,128)(2,1)} %bitcast.124), calls=%async_computation.4 | async-start | bytes 16384 | tf_op jit(solution)/shard_map/all_to_all | solution.py:180
  124.2 2.0 %bitcast_dynamic-update-slice_fusion = f32[1,128,32,128]{3,2,1,0:T(8,128)} fusion(f32[1,128,32,128]{3,2,1,0:T(8,128)} %copy.221, s32[]{:T(128)S(6)} %select_n.28, f32[128,2,128]{2,0,1:T(8,128)S(1)} %bitcast.133, f32[128,32,128]{2,1,0:T(8,128)} %bitcast.127, f32[128,2]{1,0:T(8,128)S(1)} %copy.166, f32[128,2]{1,0:T(8,128)S(1)} %copy.162), kind=kLoop, calls=%fused_computation.32 | loop fusion | flops 98304 | bytes 395268 | tf_op jit(solution)/shard_map/dynamic_update_slice | solution.py:174
  126.3 1.8 convert_element_type.130
  129.5 2.3 %all-to-all-done.4 = bf16[16,2,128]{2,1,0:T(2,128)(2,1)S(1)} async-done(((bf16[16,2,128]{2,1,0:T(2,128)(2,1)}), bf16[16,2,128]{2,1,0:T(2,128)(2,1)S(1)}, u32[]{:S(2)}, u32[]{:S(2)}) %all-to-all-start.4) | async-done | bytes 8224 | tf_op jit(solution)/shard_map/all_to_all | solution.py:180
  131.7 5.0 %all-to-all-start.2 = ((bf16[1,128,32,128]{3,1,0,2:T(8,128)(2,1)}), bf16[1,128,32,128]{3,1,0,2:T(8,128)(2,1)S(1)}, u32[]{:S(2)}, u32[]{:S(2)}) async-start(bf16[1,128,32,128]{3,1,0,2:T(8,128)(2,1)} %copy.168), calls=%async_computation.2 | async-start | bytes 2097152 | tf_op jit(solution)/shard_map/all_to_all | solution.py:187
  142.5 10.1 %all-to-all-done.2 = bf16[1,128,32,128]{3,1,0,2:T(8,128)(2,1)S(1)} async-done(((bf16[1,128,32,128]{3,1,0,2:T(8,128)(2,1)}), bf16[1,128,32,128]{3,1,0,2:T(8,128)(2,1)S(1)}, u32[]{:S(2)}, u32[]{:S(2)}) %all-to-all-start.2) | async-done | bytes 1048608 | tf_op jit(solution)/shard_map/all_to_all | solution.py:187
  154.3 2.1 %convolution_convert_fusion = bf16[128,4096]{1,0:T(8,128)(2,1)S(1)} fusion(bf16[128,256]{0,1:T(8,128)(2,1)S(1)} %bitcast.137, bf16[256,4096]{1,0:T(8,128)(2,1)} %all-gather.5.cloned.1.call-done), kind=kOutput, calls=%fused_computation.1 | convolution fusion | flops 268959744 | bytes 3211264 | tf_op jit(solution)/shard_map/dot_general | solution.py:197
  157.5 3.7 %all-to-all-start.5 = ((bf16[16,128,256]{2,1,0:T(8,128)(2,1)}), bf16[16,128,256]{2,1,0:T(8,128)(2,1)S(1)}, u32[]{:S(2)}, u32[]{:S(2)}) async-start(bf16[16,128,256]{2,1,0:T(8,128)(2,1)} %bitcast.131), calls=%async_computation.5 | async-start | bytes 2097152 | tf_op jit(solution)/shard_map/all_to_all | solution.py:33
  161.1 1.6 copy.182
  163.3 13.6 %all-to-all-done.5 = bf16[16,128,256]{2,1,0:T(8,128)(2,1)S(1)} async-done(((bf16[16,128,256]{2,1,0:T(8,128)(2,1)}), bf16[16,128,256]{2,1,0:T(8,128)(2,1)S(1)}, u32[]{:S(2)}, u32[]{:S(2)}) %all-to-all-start.5) | async-done | bytes 1048608 | tf_op jit(solution)/shard_map/all_to_all | solution.py:33
  (98 shorter events, 47.8 us)
Async XLA Ops:
  7.2 85.5 %copy-start = (bf16[2,128,4096]{2,1,0:T(8,128)(2,1)S(1)}, bf16[2,128,4096]{2,1,0:T(8,128)(2,1)}, u32[]{:S(2)}) copy-start(bf16[2,128,4096]{2,1,0:T(8,128)(2,1)} %param.17) | copy-start | bytes 6291460
  7.2 45.8 %all-gather.3.cloned.1.call-start = ((), (), s32[]{:S(2)}) async-start(), calls=%async_computation.6 | async-start | bytes 7077888 | tf_op jit(solution)/shard_map/all_gather | solution.py:107
  10.1 11.4 %copy-start.10 = (s32[2]{0:T(128)S(1)}, s32[2]{0:T(128)}, u32[]{:S(2)}) copy-start(s32[2]{0:T(128)} %param.19) | copy-start | bytes 28
  12.6 26.0 %all-to-all-start = ((bf16[16,128,256]{2,1,0:T(8,128)(2,1)}), bf16[16,128,256]{2,1,0:T(8,128)(2,1)}, u32[]{:S(2)}, u32[]{:S(2)}) async-start(bf16[16,128,256]{2,1,0:T(8,128)(2,1)} %broadcast_in_dim.95), calls=%async_computation | async-start | bytes 2097152 | tf_op jit(solution)/shard_map/all_to_all | solution.py:19
  20.8 20.0 %copy-start.7 = (f32[4096]{0:T(1024)S(1)}, f32[4096]{0:T(1024)}, u32[]{:S(2)}) copy-start(f32[4096]{0:T(1024)} %param.14) | copy-start | bytes 49156
  20.8 133.5 %all-gather.5.cloned.1.call-start = ((), (), s32[]{:S(2)}) async-start(), calls=%async_computation.7 | async-start | bytes 2359296 | tf_op jit(solution)/shard_map/all_gather | solution.py:108
  57.5 0.6 copy-start.3
  57.5 1.2 copy-start.4
  57.5 1.2 copy-start.5
  57.5 1.2 copy-start.6
  59.9 29.8 %all-to-all-start.1 = ((bf16[16,128,256]{2,1,0:T(8,128)(2,1)}), bf16[16,128,256]{2,1,0:T(8,128)(2,1)S(1)}, u32[]{:S(2)}, u32[]{:S(2)}) async-start(bf16[16,128,256]{2,1,0:T(8,128)(2,1)} %broadcast_in_dim.96), calls=%async_computation.1 | async-start | bytes 2097152 | tf_op jit(solution)/shard_map/all_to_all | solution.py:19
  89.7 3.0 %copy-start.9 = (pred[2,128]{1,0:T(4,128)(4,1)S(1)}, pred[2,128]{1,0:T(4,128)(4,1)}, u32[]{:S(2)}) copy-start(pred[2,128]{1,0:T(4,128)(4,1)} %broadcast_compare_fusion) | copy-start | bytes 772
  99.2 17.9 %all-to-all-start.3 = ((bf16[16,2,128]{2,1,0:T(2,128)(2,1)}), bf16[16,2,128]{2,1,0:T(2,128)(2,1)S(1)}, u32[]{:S(2)}, u32[]{:S(2)}) async-start(bf16[16,2,128]{2,1,0:T(2,128)(2,1)} %bitcast.125), calls=%async_computation.3 | async-start | bytes 16384 | tf_op jit(solution)/shard_map/all_to_all | solution.py:177
  106.4 4.3 %copy-start.8 = (f32[128,2]{0,1:T(2,128)S(1)}, f32[128,2]{0,1:T(2,128)}, u32[]{:S(2)}) copy-start(f32[128,2]{0,1:T(2,128)} %reshape.234) | copy-start | bytes 3076
  114.4 1.3 copy-start.1
  115.7 8.6 %copy-start.2 = (f32[2,64,2,128]{3,1,0,2:T(8,128)S(1)}, f32[2,64,2,128]{3,1,0,2:T(8,128)}, u32[]{:S(2)}) copy-start(f32[2,64,2,128]{3,1,0,2:T(8,128)} %copy.165) | copy-start | bytes 393220
  117.0 14.7 %all-to-all-start.4 = ((bf16[16,2,128]{2,1,0:T(2,128)(2,1)}), bf16[16,2,128]{2,1,0:T(2,128)(2,1)S(1)}, u32[]{:S(2)}, u32[]{:S(2)}) async-start(bf16[16,2,128]{2,1,0:T(2,128)(2,1)} %bitcast.124), calls=%async_computation.4 | async-start | bytes 16384 | tf_op jit(solution)/shard_map/all_to_all | solution.py:180
  131.7 20.9 %all-to-all-start.2 = ((bf16[1,128,32,128]{3,1,0,2:T(8,128)(2,1)}), bf16[1,128,32,128]{3,1,0,2:T(8,128)(2,1)S(1)}, u32[]{:S(2)}, u32[]{:S(2)}) async-start(bf16[1,128,32,128]{3,1,0,2:T(8,128)(2,1)} %copy.168), calls=%async_computation.2 | async-start | bytes 2097152 | tf_op jit(solution)/shard_map/all_to_all | solution.py:187
  157.5 19.5 %all-to-all-start.5 = ((bf16[16,128,256]{2,1,0:T(8,128)(2,1)}), bf16[16,128,256]{2,1,0:T(8,128)(2,1)S(1)}, u32[]{:S(2)}, u32[]{:S(2)}) async-start(bf16[16,128,256]{2,1,0:T(8,128)(2,1)} %bitcast.131), calls=%async_computation.5 | async-start | bytes 2097152 | tf_op jit(solution)/shard_map/all_to_all | solution.py:33
Sparse Core Ops, SparseCore 0:
  9.7 43.2 all-gather.2
  54.7 25.3 all-gather.4
where the time goes:
time: 186 us; the launch traced here: 185 us
  waiting for transfers between devices  54.7 us (29%)
  local copies, waits for them, and re-layouts  42.2 us (23%)
  starting transfers between devices  38.4 us (21%)
  matrix products  17.7 us (10%)
  other arithmetic  17.1 us (9%)
  between operations  14.4 us (8%)
    all_to_all x2, waiting for transfers between devices, from_everyone(): lax.all_to_all(jnp.broadcast_to(x[None], (count, *x.shape)), axis, 0, 0,...  16.7 us
    all_to_all x2, starting transfers between devices, from_everyone(): lax.all_to_all(jnp.broadcast_to(x[None], (count, *x.shape)), axis, 0, 0,...  15.2 us
    all_to_all x1, waiting for transfers between devices, summed_on_arrival(): blocks = lax.all_to_all(cut_along(x, dim, count), axis, 0, 0, tiled=True)  13.6 us
    concatenate x8, local copies, waits for them, and re-layouts, rotate(): jnp.concatenate([first * cosine - second * sine, second * cosine + first...  12.1 us
    all_gather x1, waiting for transfers between devices, shards(): lax.all_gather(qkv_weight, 'wt', axis=0, tiled=True)  10.7 us
    all_to_all x1, waiting for transfers between devices, shards(): lax.all_to_all(part_numer[None].astype(jnp.bfloat16), 'ctx', split_axis=2...  10.1 us
    all_to_all x1, starting transfers between devices, shards(): lax.all_to_all(part_total[None].astype(jnp.bfloat16), 'ctx', split_axis=2...  7.21 us
    all_to_all x1, starting transfers between devices, shards(): lax.all_to_all(part_max[None].astype(jnp.bfloat16), 'ctx', split_axis=2,...  7.21 us
  transfers between devices with their start and end apart: 8, of which 5 were waited for; matrix products, arithmetic and copies ran while one was open for 39% of the time, Pallas kernels for 0%

commit v1 on v0

--- a/solution.py
+++ b/solution.py
@@ -6,6 +6,11 @@
 HEADS = 32
 HEAD = 128
 FLOOR_SCORE = -1e30
+
+
+def all_by_exchange(block, name, dim):
+    sent = jnp.stack([block] * lax.axis_size(name))
+    return jnp.concatenate(lax.all_to_all(sent, name, 0, 0), axis=dim)
 
 
 def in_order(blocks, dim):
@@ -104,7 +109,7 @@
         wide * lax.rsqrt(jnp.mean(wide * wide, axis=-1, keepdims=True) + 1e-06) * norm_gain
     ).astype(jnp.bfloat16)
     qkv_full, out_rows = (
-        lax.all_gather(qkv_weight, "wt", axis=0, tiled=True),
+        all_by_exchange(qkv_weight, "wt", 0),
         lax.all_gather(out_weight, "wt", axis=1, tiled=True),
     )
     projected = jnp.einsum("rd,dke->rke", normed, qkv_full, preferred_element_type=jnp.float32)

time: 186 us -> 255 us (1.37)
  waiting for transfers between devices: 54.7 us -> 101 us
  blocking collectives: 0 us -> 24.9 us
  starting transfers between devices: 38.4 us -> 31.9 us
  local copies, waits for them, and re-layouts: 42.2 us -> 47.8 us
  matrix products: 17.7 us -> 14.8 us
    all_to_all x0 -> x1, waiting for transfers between devices: none -> 75.1 us  [all_by_exchange(): return jnp.concatenate(lax.all_to_all(sent, name, 0, 0), axis=dim)]
    all_to_all x0 -> x1, blocking collectives: none -> 24.9 us  [from_everyone(): lax.all_to_all(jnp.broadcast_to(x[None], (count, *x.shape)), axis, 0, 0,...]
    all_to_all x2 -> x1, waiting for transfers between devices: 16.7 us -> 0.01 us  [from_everyone(): lax.all_to_all(jnp.broadcast_to(x[None], (count, *x.shape)), axis, 0, 0,...]
    all_to_all x2 -> x1, starting transfers between devices: 15.2 us -> 3.85 us  [from_everyone(): lax.all_to_all(jnp.broadcast_to(x[None], (count, *x.shape)), axis, 0, 0,...]
    all_gather x1 -> x0, waiting for transfers between devices: 10.7 us -> none  [shards(): lax.all_gather(qkv_weight, 'wt', axis=0, tiled=True)]
    all_to_all x0 -> x1, starting transfers between devices: none -> 4.87 us  [all_by_exchange(): return jnp.concatenate(lax.all_to_all(sent, name, 0, 0), axis=dim)]
    another operation x0 -> x1, local copies, waits for them, and re-layouts: none -> 3.33 us  [all_by_exchange(): sent = jnp.stack([block] * lax.axis_size(name))]
    all_to_all x0 -> x1, local copies, waits for them, and re-layouts: none -> 3.2 us  [all_by_exchange(): return jnp.concatenate(lax.all_to_all(sent, name, 0, 0), axis=dim)]
  transfers between devices with their start and end apart: 8 -> 7, of which waited for: 5 -> 4; matrix products, arithmetic and copies ran while one was open for 39% -> 27% of each run, Pallas kernels for 0% -> 0%
where the time goes in v1:
time: 255 us; the launch traced here: 254 us
  waiting for transfers between devices  101 us (40%)
  local copies, waits for them, and re-layouts  47.8 us (19%)
  starting transfers between devices  31.9 us (13%)
  blocking collectives  24.9 us (10%)
  other arithmetic  18.6 us (7%)
  matrix products  14.8 us (6%)
  between operations  14.4 us (6%)
    all_to_all x1, waiting for transfers between devices, all_by_exchange(): return jnp.concatenate(lax.all_to_all(sent, name, 0, 0), axis=dim)  75.1 us
    all_to_all x1, blocking collectives, from_everyone(): lax.all_to_all(jnp.broadcast_to(x[None], (count, *x.shape)), axis, 0, 0,...  24.9 us
    all_to_all x1, waiting for transfers between devices, summed_on_arrival(): blocks = lax.all_to_all(cut_along(x, dim, count), axis, 0, 0, tiled=True)  13.7 us
    concatenate x8, local copies, waits for them, and re-layouts, rotate(): jnp.concatenate([first * cosine - second * sine, second * cosine + first...  12.2 us
    all_to_all x1, waiting for transfers between devices, shards(): lax.all_to_all(part_numer[None].astype(jnp.bfloat16), 'ctx', split_axis=2...  9.43 us
    all_to_all x1, starting transfers between devices, shards(): lax.all_to_all(part_total[None].astype(jnp.bfloat16), 'ctx', split_axis=2...  7.21 us
    all_to_all x1, starting transfers between devices, shards(): lax.all_to_all(part_max[None].astype(jnp.bfloat16), 'ctx', split_axis=2,...  7.21 us
    unnamed x32, local copies, waits for them, and re-layouts  6.43 us
  transfers between devices with their start and end apart: 7, of which 4 were waited for; matrix products, arithmetic and copies ran while one was open for 27% of the time, Pallas kernels for 0%

profile of v1, /device:TPU:0, one launch (start us, length us, event | category | flops | bytes accessed | tf_op | source)
XLA Modules:
  0.0 253.6 jit_solution(15471865690593958988)
XLA Ops:
  11.1 24.9 %all_to_all.53 = bf16[16,128,256]{2,1,0:T(8,128)(2,1)} all-to-all(bf16[16,128,256]{2,1,0:T(8,128)(2,1)S(1)} %broadcast_in_dim.95), channel_id=1, replica_groups=mesh['ctx'=16,'wt'=8] {'ctx'}, dimensions={0} | all-to-all | bytes 2097152 | tf_op jit(solution)/shard_map/all_to_all | solution.py:24
  36.0 3.3 %stack.2 = bf16[8,512,3,256]{3,1,2,0:T(8,128)(2,1)} broadcast(bf16[512,3,256]{2,0,1:T(8,128)(2,1)S(1)} %copy-done.3), dimensions={1,2,3} | broadcast | bytes 7077888 | tf_op jit(solution)/shard_map/stack | solution.py:12
  39.3 4.9 %all-to-all-start.1 = ((bf16[8,512,3,256]{3,1,2,0:T(8,128)(2,1)}), bf16[8,512,3,256]{3,1,2,0:T(8,128)(2,1)}, u32[]{:S(2)}, u32[]{:S(2)}) async-start(bf16[8,512,3,256]{3,1,2,0:T(8,128)(2,1)} %stack.2), calls=%async_computation.1 | async-start | bytes 12582912 | tf_op jit(solution)/shard_map/all_to_all | solution.py:13
  46.0 1.6 copy.146
  49.7 75.1 %all-to-all-done.1 = bf16[8,512,3,256]{3,1,2,0:T(8,128)(2,1)} async-done(((bf16[8,512,3,256]{3,1,2,0:T(8,128)(2,1)}), bf16[8,512,3,256]{3,1,2,0:T(8,128)(2,1)}, u32[]{:S(2)}, u32[]{:S(2)}) %all-to-all-start.1) | async-done | bytes 6291488 | tf_op jit(solution)/shard_map/all_to_all | solution.py:13
  124.8 3.2 %copy.147 = bf16[8,512,3,256]{3,1,0,2:T(8,128)(2,1)S(1)} copy(bf16[8,512,3,256]{3,1,2,0:T(8,128)(2,1)} %all-to-all-done.1) | data formatting | bytes 12582912 | tf_op jit(solution)/shard_map/all_to_all | solution.py:13
  132.6 3.8 %all-to-all-start.2 = ((bf16[16,128,256]{2,1,0:T(8,128)(2,1)}), bf16[16,128,256]{2,1,0:T(8,128)(2,1)S(1)}, u32[]{:S(2)}, u32[]{:S(2)}) async-start(bf16[16,128,256]{2,1,0:T(8,128)(2,1)} %broadcast_in_dim.96), calls=%async_computation.2 | async-start | bytes 2097152 | tf_op jit(solution)/shard_map/all_to_all | solution.py:24
  146.1 1.6 copy.163
  149.2 1.8 select_reduce_fusion.1
  162.2 2.9 %select_reduce_fusion = (f32[2,32,64]{2,1,0:T(8,128)S(1)}, f32[2,32,64,128]{3,2,1,0:T(8,128)}) fusion(pred[2,128]{1,0:T(4,128)(4,1)S(1)} %copy-done.11, bf16[2,64,32,128]{3,2,1,0:T(8,128)(2,1)S(1)} %reshape_reshape.3, bf16[2,128,4096]{2,1,0:T(8,128)(2,1)S(1)} %copy-done), kind=kOutput, calls=%fused_computation.16 | convolution fusion | flops 135786496 | bytes 5259520 | tf_op jit(solution)/shard_map/mthd,mphd->mhtp/dot_general | solution.py:131
  165.3 2.5 %fusion.13 = f32[2,32,64]{2,1,0:T(8,128)S(1)} fusion(f32[2,32,64,128]{3,2,1,0:T(8,128)} %get-tuple-element.21, f32[2,32,64]{2,1,0:T(8,128)S(1)} %get-tuple-element.15, pred[2,128]{1,0:T(4,128)(4,1)S(1)} %copy-done.11), kind=kLoop, calls=%fused_computation.18 | loop fusion | flops 2093056 | bytes 2130176 | tf_op jit(solution)/shard_map/reduce_sum | solution.py:138
  168.7 7.2 %all-to-all-start.4 = ((bf16[16,2,128]{2,1,0:T(2,128)(2,1)}), bf16[16,2,128]{2,1,0:T(2,128)(2,1)S(1)}, u32[]{:S(2)}, u32[]{:S(2)}) async-start(bf16[16,2,128]{2,1,0:T(2,128)(2,1)} %bitcast.121), calls=%async_computation.4 | async-start | bytes 16384 | tf_op jit(solution)/shard_map/all_to_all | solution.py:182
  175.9 4.3 %fusion.10 = f32[2,64,32,128]{3,1,2,0:T(8,128)} fusion(f32[2,32,64,128]{3,2,1,0:T(8,128)} %get-tuple-element.21, f32[2,32,64]{2,1,0:T(8,128)S(1)} %get-tuple-element.15, pred[2,128]{1,0:T(4,128)(4,1)S(1)} %copy-done.11, bf16[2,128,4096]{2,1,0:T(8,128)(2,1)} %param.18), kind=kOutput, calls=%fused_computation.17 | convolution fusion | flops 136314880 | bytes 6308096 | tf_op jit(solution)/shard_map/mhtp,mphd->mthd/dot_general | solution.py:139
  181.1 2.8 %copy.156 = f32[2,64,32,128]{3,2,1,0:T(8,128)S(1)} copy(f32[2,64,32,128]{3,1,2,0:T(8,128)} %fusion.10) | data formatting | bytes 4194304 | tf_op jit(solution)/shard_map/mhtp,mphd->mthd/transpose | solution.py:139
  186.5 7.2 %all-to-all-start.5 = ((bf16[16,2,128]{2,1,0:T(2,128)(2,1)}), bf16[16,2,128]{2,1,0:T(2,128)(2,1)S(1)}, u32[]{:S(2)}, u32[]{:S(2)}) async-start(bf16[16,2,128]{2,1,0:T(2,128)(2,1)} %bitcast.120), calls=%async_computation.5 | async-start | bytes 16384 | tf_op jit(solution)/shard_map/all_to_all | solution.py:185
  193.8 2.0 bitcast_dynamic-update-slice_fusion
  195.8 1.8 convert_element_type.128
  199.0 2.3 all-to-all-done.5
  201.3 5.0 %all-to-all-start.3 = ((bf16[1,128,32,128]{3,1,0,2:T(8,128)(2,1)}), bf16[1,128,32,128]{3,1,0,2:T(8,128)(2,1)S(1)}, u32[]{:S(2)}, u32[]{:S(2)}) async-start(bf16[1,128,32,128]{3,1,0,2:T(8,128)(2,1)} %copy.172), calls=%async_computation.3 | async-start | bytes 2097152 | tf_op jit(solution)/shard_map/all_to_all | solution.py:192
  212.0 9.4 %all-to-all-done.3 = bf16[1,128,32,128]{3,1,0,2:T(8,128)(2,1)S(1)} async-done(((bf16[1,128,32,128]{3,1,0,2:T(8,128)(2,1)}), bf16[1,128,32,128]{3,1,0,2:T(8,128)(2,1)S(1)}, u32[]{:S(2)}, u32[]{:S(2)}) %all-to-all-start.3) | async-done | bytes 1048608 | tf_op jit(solution)/shard_map/all_to_all | solution.py:192
  223.2 2.1 convolution_convert_fusion
  226.3 3.7 %all-to-all-start.6 = ((bf16[16,128,256]{2,1,0:T(8,128)(2,1)}), bf16[16,128,256]{2,1,0:T(8,128)(2,1)S(1)}, u32[]{:S(2)}, u32[]{:S(2)}) async-start(bf16[16,128,256]{2,1,0:T(8,128)(2,1)} %bitcast.128), calls=%async_computation.6 | async-start | bytes 2097152 | tf_op jit(solution)/shard_map/all_to_all | solution.py:38
  230.0 1.6 copy.186
  232.2 13.7 %all-to-all-done.6 = bf16[16,128,256]{2,1,0:T(8,128)(2,1)S(1)} async-done(((bf16[16,128,256]{2,1,0:T(8,128)(2,1)}), bf16[16,128,256]{2,1,0:T(8,128)(2,1)S(1)}, u32[]{:S(2)}, u32[]{:S(2)}) %all-to-all-start.6) | async-done | bytes 1048608 | tf_op jit(solution)/shard_map/all_to_all | solution.py:38
  (103 shorter events, 50.3 us)
Async XLA Ops:
  7.2 155.0 %copy-start = (bf16[2,128,4096]{2,1,0:T(8,128)(2,1)S(1)}, bf16[2,128,4096]{2,1,0:T(8,128)(2,1)}, u32[]{:S(2)}) copy-start(bf16[2,128,4096]{2,1,0:T(8,128)(2,1)} %param.17) | copy-start | bytes 6291460
  9.5 26.5 %copy-start.3 = (bf16[512,3,256]{2,0,1:T(8,128)(2,1)S(1)}, bf16[512,3,256]{2,0,1:T(8,128)(2,1)}, u32[]{:S(2)}) copy-start(bf16[512,3,256]{2,0,1:T(8,128)(2,1)} %param.15) | copy-start | bytes 2359300
  39.3 5.6 %copy-start.9 = (f32[4096]{0:T(1024)S(1)}, f32[4096]{0:T(1024)}, u32[]{:S(2)}) copy-start(f32[4096]{0:T(1024)} %param.14) | copy-start | bytes 49156
  39.3 5.6 %copy-start.12 = (s32[2]{0:T(128)S(1)}, s32[2]{0:T(128)}, u32[]{:S(2)}) copy-start(s32[2]{0:T(128)} %param.19) | copy-start | bytes 28
  39.3 85.4 %all-to-all-start.1 = ((bf16[8,512,3,256]{3,1,2,0:T(8,128)(2,1)}), bf16[8,512,3,256]{3,1,2,0:T(8,128)(2,1)}, u32[]{:S(2)}, u32[]{:S(2)}) async-start(bf16[8,512,3,256]{3,1,2,0:T(8,128)(2,1)} %stack.2), calls=%async_computation.1 | async-start | bytes 12582912 | tf_op jit(solution)/shard_map/all_to_all | solution.py:13
  44.2 179.0 %all-gather.2.cloned.1.call-start = ((), (), s32[]{:S(2)}) async-start(), calls=%async_computation.7 | async-start | bytes 2359296 | tf_op jit(solution)/shard_map/all_gather | solution.py:113
  49.7 78.3 %copy-start.2 = (bf16[16,128,256]{1,2,0:T(8,128)(2,1)S(1)}, bf16[16,128,256]{1,2,0:T(8,128)(2,1)}, u32[]{:S(2)}) copy-start(bf16[16,128,256]{1,2,0:T(8,128)(2,1)} %fusion.2) | copy-start | bytes 3145732
  130.1 0.6 copy-start.5
  130.1 1.2 copy-start.6
  130.1 1.2 copy-start.7
  130.2 1.2 copy-start.8
  132.6 26.6 %all-to-all-start.2 = ((bf16[16,128,256]{2,1,0:T(8,128)(2,1)}), bf16[16,128,256]{2,1,0:T(8,128)(2,1)S(1)}, u32[]{:S(2)}, u32[]{:S(2)}) async-start(bf16[16,128,256]{2,1,0:T(8,128)(2,1)} %broadcast_in_dim.96), calls=%async_computation.2 | async-start | bytes 2097152 | tf_op jit(solution)/shard_map/all_to_all | solution.py:24
  159.2 3.0 %copy-start.11 = (pred[2,128]{1,0:T(4,128)(4,1)S(1)}, pred[2,128]{1,0:T(4,128)(4,1)}, u32[]{:S(2)}) copy-start(pred[2,128]{1,0:T(4,128)(4,1)} %broadcast_compare_fusion) | copy-start | bytes 772
  168.7 17.9 %all-to-all-start.4 = ((bf16[16,2,128]{2,1,0:T(2,128)(2,1)}), bf16[16,2,128]{2,1,0:T(2,128)(2,1)S(1)}, u32[]{:S(2)}, u32[]{:S(2)}) async-start(bf16[16,2,128]{2,1,0:T(2,128)(2,1)} %bitcast.121), calls=%async_computation.4 | async-start | bytes 16384 | tf_op jit(solution)/shard_map/all_to_all | solution.py:182
  175.9 4.3 %copy-start.10 = (f32[128,2]{0,1:T(2,128)S(1)}, f32[128,2]{0,1:T(2,128)}, u32[]{:S(2)}) copy-start(f32[128,2]{0,1:T(2,128)} %reshape.249) | copy-start | bytes 3076
  183.9 1.3 copy-start.1
  185.2 8.6 %copy-start.4 = (f32[2,64,2,128]{3,1,0,2:T(8,128)S(1)}, f32[2,64,2,128]{3,1,0,2:T(8,128)}, u32[]{:S(2)}) copy-start(f32[2,64,2,128]{3,1,0,2:T(8,128)} %copy.169) | copy-start | bytes 393220
  186.5 14.7 %all-to-all-start.5 = ((bf16[16,2,128]{2,1,0:T(2,128)(2,1)}), bf16[16,2,128]{2,1,0:T(2,128)(2,1)S(1)}, u32[]{:S(2)}, u32[]{:S(2)}) async-start(bf16[16,2,128]{2,1,0:T(2,128)(2,1)} %bitcast.120), calls=%async_computation.5 | async-start | bytes 16384 | tf_op jit(solution)/shard_map/all_to_all | solution.py:185
  201.3 20.2 %all-to-all-start.3 = ((bf16[1,128,32,128]{3,1,0,2:T(8,128)(2,1)}), bf16[1,128,32,128]{3,1,0,2:T(8,128)(2,1)S(1)}, u32[]{:S(2)}, u32[]{:S(2)}) async-start(bf16[1,128,32,128]{3,1,0,2:T(8,128)(2,1)} %copy.172), calls=%async_computation.3 | async-start | bytes 2097152 | tf_op jit(solution)/shard_map/all_to_all | solution.py:192
  226.3 19.6 %all-to-all-start.6 = ((bf16[16,128,256]{2,1,0:T(8,128)(2,1)}), bf16[16,128,256]{2,1,0:T(8,128)(2,1)S(1)}, u32[]{:S(2)}, u32[]{:S(2)}) async-start(bf16[16,128,256]{2,1,0:T(8,128)(2,1)} %bitcast.128), calls=%async_computation.6 | async-start | bytes 2097152 | tf_op jit(solution)/shard_map/all_to_all | solution.py:38
Sparse Core Ops, SparseCore 0:
  46.7 33.4 all-gather.1
